TPU v7x, 128 devices: a whole 4x4x4 slice. The times are simulated.
128 devices in a mesh: pair: 8 (over x, core), aux: 16 (over y, z).
Axes of the slice: x: 4, y: 4, z: 4, core: 2. Of those that a mesh axis runs over, the one named last changes fastest.
Arguments:
- left_active: bfloat16 [80, 128, 61440], P('pair', None, 'aux'), may hold values from -0.375 to 0.375
- right_active: bfloat16 [80, 128, 61440], P('pair', None, 'aux'), may hold values from -0.375 to 0.375
- amps_active: bfloat16 [80, 128, 128], P('pair', 'aux'), may hold values from -0.5 to 0.5
- rank_active: int32 [80], P('pair'), may hold values from 80 to 128, as said below
- gap_active: float32 [80], P('pair'), may hold values from 0.5 to 2
- energy_active: float32 [80, 128], P('pair'), may hold values from 0.5 to 4
- intersect_active: bfloat16 [80, 4, 128, 128], P('pair'), may hold values from -0.75 to 0.75
- fock_active: float32 [80, 4], P('pair'), may hold values from -2 to 2
- neighbor_active: int32 [80, 4], P('pair'), may hold values from 0 to 79
- left_env: bfloat16 [32, 48, 61440], P('pair', None, 'aux'), may hold values from -0.375 to 0.375
- right_env: bfloat16 [32, 48, 61440], P('pair', None, 'aux'), may hold values from -0.375 to 0.375
- amps_env: bfloat16 [32, 48, 48], P('pair', 'aux'), may hold values from -0.875 to 0.875
- rank_env: int32 [32], P('pair'), may hold values from 24 to 48, as said below
- gap_env: float32 [32], P('pair'), may hold values from 0.5 to 2
- energy_env: float32 [32, 48], P('pair'), may hold values from 0.5 to 4
- intersect_env: bfloat16 [32, 4, 48, 48], P('pair'), may hold values from -1.25 to 1.25
- fock_env: float32 [32, 4], P('pair'), may hold values from -2 to 2
- neighbor_env: int32 [32, 4], P('pair'), may hold values from 0 to 31
Outputs:
- new_active: float32 [80, 128, 128], P('pair', 'aux')
- new_env: float32 [32, 48, 48], P('pair', 'aux')
Inputs may be any that keep to these rules, and one draw needn't show every extreme that they name: `rank_active`: multiples of 8; the first active pair has rank 128. `rank_env`: multiples of 8; the first environment pair has rank 48.
All inputs are finite; a program needn't handle non-finite values.
Results may differ from a plain program's by a relative error of at most 0.0041.
Values may be sent and summed in bfloat16 or wider, within the bound.
A program may use at most 128 MiB of HBM per device.

v0:
```python
import functools

import jax
import jax.numpy as jnp
from jax import lax
from jax.experimental import pallas as pl
from jax.experimental.pallas import tpu as pltpu
from jax.sharding import PartitionSpec as P

MESH = pl.DeviceIdType.MESH
F32, BF16 = jnp.float32, jnp.bfloat16
AHEAD = 3
LANES, SUBS = 128, 8


def shard_mask(pair_ranks, row_count, full_width, row_start):
    row_index = row_start + jnp.arange(row_count, dtype=jnp.int32)
    col_index = jnp.arange(full_width, dtype=jnp.int32)
    return (row_index[None, :, None] < pair_ranks[:, None, None]) & (
        col_index[None, None, :] < pair_ranks[:, None, None]
    )


def finish(summed, amp_shard, pair_ranks, pair_gaps, energy, row_start):
    row_count = amp_shard.shape[1]
    inside = shard_mask(pair_ranks, row_count, amp_shard.shape[2], row_start)
    energy_rows = lax.dynamic_slice_in_dim(energy, row_start, row_count, 1)
    denominator = energy_rows[:, :, None] + energy[:, None, :] + pair_gaps[:, None, None]
    return jnp.where(inside, amp_shard.astype(F32) - summed / denominator, F32(0.0))


def halves(x):
    high = x.astype(BF16)
    return high, (x - high.astype(F32)).astype(BF16)


def dot(a, b, ca, cb):
    return lax.dot_general(a, b, (((ca,), (cb,)), ((), ())), preferred_element_type=F32)


def masked_rows(amps, rank, start):
    row = start + lax.broadcasted_iota(jnp.int32, amps.shape, 0)
    col = lax.broadcasted_iota(jnp.int32, amps.shape, 1)
    return jnp.where((row < rank) & (col < rank), amps.astype(F32), 0.0)


def kernel(
    npair, naux,
    nbr_a, rank_a, fock_a, nbr_e, rank_e, fock_e, amps_a, amps_e,
    la_hbm, ra_hbm, sa_hbm, le_hbm, re_hbm, se_hbm,
    out_a, out_e,
    la, ra, sa, le, re, se, gat, blk_a, blk_e, near, part_e,
    send_a, recv_a, send_e, recv_e, first_a,
    la_sem, ra_sem, le_sem, re_sem, sa_sem, se_sem,
    gat_s, gat_r, blk_s, blk_r, ble_s, ble_r, rsa_s, rsa_r, rse_s, rse_r,
):
    me, grp = lax.axis_index("aux"), lax.axis_index("pair")
    count_a, rows_a, wide_a = amps_a.shape
    count_e, rows_e, wide_e = amps_e.shape
    nb = nbr_a.shape[1]
    start_a, start_e = me * rows_a, me * rows_e

    def load_pair(p):
        return (
            pltpu.make_async_copy(la_hbm.at[p], la.at[p], la_sem.at[p]),
            pltpu.make_async_copy(ra_hbm.at[p], ra.at[p], ra_sem.at[p]),
        )

    load_env = (
        pltpu.make_async_copy(le_hbm, le, le_sem),
        pltpu.make_async_copy(re_hbm, re, re_sem),
    )
    load_over = (
        pltpu.make_async_copy(se_hbm, se, se_sem),
        pltpu.make_async_copy(sa_hbm, sa, sa_sem),
    )
    for copy in load_env + load_pair(0) + load_over:
        copy.start()
    for p in range(1, min(AHEAD, count_a)):
        for copy in load_pair(p):
            copy.start()

    barrier = pltpu.get_barrier_semaphore()

    @pl.loop(1, naux)
    def _(d):
        pl.semaphore_signal(
            barrier, inc=1, device_id={"aux": lax.rem(me + d, naux)}, device_id_type=MESH
        )

    @pl.loop(1, npair)
    def _(d):
        pl.semaphore_signal(
            barrier, inc=1, device_id={"pair": lax.rem(grp + d, npair)}, device_id_type=MESH
        )

    @pl.loop(0, count_a)
    def _(p):
        own = masked_rows(amps_a[p], rank_a[p], start_a).astype(BF16)
        gat[me, p] = own
        blk_a[grp * count_a + p] = own

    for q in range(count_e):
        own = masked_rows(amps_e[q], rank_e[q], start_e)
        row = lax.broadcasted_iota(jnp.int32, (wide_e, wide_e), 0)
        placed = jnp.zeros((wide_e, wide_e), F32)
        for i in range(rows_e):
            placed = jnp.where(row == start_e + i, own[i : i + 1, :], placed)
        at = grp * count_e + q
        blk_e[at] = jnp.zeros(blk_e.shape[1:], BF16)
        blk_e[at, :, :wide_e] = placed.astype(BF16)
    near[...] = jnp.zeros_like(near)
    send_e[...] = jnp.zeros_like(send_e)
    pl.semaphore_wait(barrier, naux + npair - 2)

    def to_aux(d):
        slot = gat.at[me]
        return pltpu.make_async_remote_copy(
            src_ref=slot, dst_ref=slot, send_sem=gat_s.at[d], recv_sem=gat_r.at[d],
            device_id={"aux": lax.rem(me + d, naux)}, device_id_type=MESH,
        )

    def to_pair(d, block, count, s, r):
        slot = block.at[pl.ds(grp * count, count)]
        return pltpu.make_async_remote_copy(
            src_ref=slot, dst_ref=slot, send_sem=s.at[d], recv_sem=r.at[d],
            device_id={"pair": lax.rem(grp + d, npair)}, device_id_type=MESH,
        )

    @pl.loop(1, naux)
    def _(d):
        to_aux(d).start()

    @pl.loop(1, npair)
    def _(d):
        to_pair(d, blk_a, count_a, blk_s, blk_r).start()
        to_pair(d, blk_e, count_e, ble_s, ble_r).start()

    def ladder(p):
        for copy in load_pair(p):
            copy.wait()
        return dot(la[p], ra[p], 1, 1)

    for copy in load_env:
        copy.wait()
    flat = (count_e * wide_e, le.shape[2])
    base_e = dot(le[...].reshape(flat), re[...].reshape(flat), 1, 1)
    first_a[...] = ladder(0)

    @pl.loop(1, npair)
    def _(d):
        to_pair(d, blk_a, count_a, blk_s, blk_r).wait()
        to_pair(d, blk_e, count_e, ble_s, ble_r).wait()

    @pl.loop(1, naux)
    def _(d):
        to_aux(d).wait()

    for copy in load_over:
        copy.wait()

    for q in range(count_e):
        lo, hi = q * wide_e, (q + 1) * wide_e
        total = base_e[lo:hi, lo:hi]
        for k in range(nb):
            over = se[q, k]
            right = dot(blk_e[nbr_e[q, k], :, :wide_e], over, 1, 1) * fock_e[q, k]
            high, low = halves(right)
            total = total + dot(over, high, 1, 0) + dot(over, low, 1, 0)
        part_e[:, :wide_e] = total
        for j in range(naux):
            send_e[j, q, :rows_e, :wide_e] = part_e[j * rows_e : (j + 1) * rows_e, :wide_e]

    def sums_env(d):
        peer = lax.rem(me + d, naux)
        return pltpu.make_async_remote_copy(
            src_ref=send_e.at[peer], dst_ref=recv_e.at[d - 1],
            send_sem=rse_s.at[d], recv_sem=rse_r.at[d],
            device_id={"aux": peer}, device_id_type=MESH,
        )

    def send_pair(p):
        @pl.loop(1, naux)
        def _(d):
            peer = lax.rem(me + d, naux)
            pltpu.make_async_remote_copy(
                src_ref=send_a.at[p, peer], dst_ref=recv_a.at[d - 1, p],
                send_sem=rsa_s.at[d], recv_sem=rsa_r.at[d],
                device_id={"aux": peer}, device_id_type=MESH,
            ).start()

    def whole_pair(p, base):
        amp = gat[:, p].astype(F32).reshape(wide_a, wide_a).astype(BF16)
        total = base
        for k in range(nb):
            over = sa[p, k]
            right = dot(blk_a[nbr_a[p, k]], over, 1, 1) * fock_a[p, k]
            at = pl.ds(pl.multiple_of(start_a, rows_a), rows_a)
            near[k, at, :] = right
            high, low = halves(near[k])
            total = total + dot(
                jnp.concatenate([over, over], axis=1), jnp.concatenate([high, low], axis=0), 1, 0
            )
        x = dot(amp, jnp.concatenate(halves(base), axis=1), 0, 0)
        x = x[:, :wide_a] + x[:, wide_a:]
        y = dot(jnp.concatenate(halves(x), axis=0), amp, 1, 1)
        total = total + x + y[:wide_a] + y[wide_a:]
        send_a[p] = total.reshape(naux, rows_a, wide_a)

    @pl.loop(0, count_a)
    def _(p):
        @pl.when(p + AHEAD < count_a)
        def _():
            for copy in load_pair(p + AHEAD):
                copy.start()

        @pl.when(p > 0)
        def _():
            first_a[...] = ladder(p)

        @pl.when(p == 0)
        def _():
            @pl.loop(1, naux)
            def _(d):
                sums_env(d).start()

        @pl.when(p > 0)
        def _():
            send_pair(p - 1)

        whole_pair(p, first_a[...])

    send_pair(count_a - 1)

    @pl.loop(1, naux)
    def _(d):
        sums_env(d).wait()

    total_e = send_e[me]
    for d in range(naux - 1):
        total_e = total_e + recv_e[d]
    out_e[...] = total_e

    @pl.loop(1, naux)
    def _(d):
        whole = recv_a.at[d - 1]
        pltpu.make_async_remote_copy(
            src_ref=whole, dst_ref=whole, send_sem=rsa_s.at[d], recv_sem=rsa_r.at[d],
            device_id={"aux": lax.rem(me + d, naux)}, device_id_type=MESH,
        ).wait()

    total_a = send_a[:, me]
    for d in range(naux - 1):
        total_a = total_a + recv_a[d]
    out_a[...] = total_a


def round_up(x, m):
    return (x + m - 1) // m * m


def shards(
    npair, naux,
    left_active, right_active, amps_active, rank_active, gap_active, energy_active,
    intersect_active, fock_active, neighbor_active,
    left_env, right_env, amps_env, rank_env, gap_env, energy_env,
    intersect_env, fock_env, neighbor_env,
):
    aux_place = lax.axis_index("aux")
    count_a, rows_a, wide_a = amps_active.shape
    count_e, rows_e, wide_e = amps_env.shape
    rows_p, wide_p = round_up(rows_e, SUBS), round_up(wide_e, LANES)
    smem = pl.BlockSpec(memory_space=pltpu.SMEM)
    vmem = pl.BlockSpec(memory_space=pltpu.VMEM)
    anyw = pl.BlockSpec(memory_space=pl.ANY)
    dma = pltpu.SemaphoreType.DMA
    total_a, total_e = pl.pallas_call(
        functools.partial(kernel, npair, naux),
        out_shape=(
            jax.ShapeDtypeStruct((count_a, rows_a, wide_a), F32),
            jax.ShapeDtypeStruct((count_e, rows_p, wide_p), F32),
        ),
        in_specs=[smem] * 6 + [vmem] * 2 + [anyw] * 6,
        out_specs=(vmem, vmem),
        scratch_shapes=[
            pltpu.VMEM(left_active.shape, BF16),
            pltpu.VMEM(right_active.shape, BF16),
            pltpu.VMEM(intersect_active.shape, BF16),
            pltpu.VMEM(left_env.shape, BF16),
            pltpu.VMEM(right_env.shape, BF16),
            pltpu.VMEM(intersect_env.shape, BF16),
            pltpu.VMEM((naux, count_a, rows_a, wide_a), BF16),
            pltpu.VMEM((npair * count_a, rows_a, wide_a), BF16),
            pltpu.VMEM((npair * count_e, wide_e, wide_p), BF16),
            pltpu.VMEM((neighbor_active.shape[1], wide_a, wide_a), F32),
            pltpu.VMEM((wide_e, wide_p), F32),
            pltpu.VMEM((count_a, naux, rows_a, wide_a), F32),
            pltpu.VMEM((naux - 1, count_a, rows_a, wide_a), F32),
            pltpu.VMEM((naux, count_e, rows_p, wide_p), F32),
            pltpu.VMEM((naux - 1, count_e, rows_p, wide_p), F32),
            pltpu.VMEM((wide_a, wide_a), F32),
            dma((count_a,)), dma((count_a,)), dma, dma, dma, dma,
            dma((naux,)), dma((naux,)),
            dma((npair,)), dma((npair,)), dma((npair,)), dma((npair,)),
            dma((naux,)), dma((naux,)), dma((naux,)), dma((naux,)),
        ],
        compiler_params=pltpu.CompilerParams(
            collective_id=0, has_side_effects=True, vmem_limit_bytes=60 * 1024 * 1024
        ),
    )(
        neighbor_active, rank_active, fock_active, neighbor_env, rank_env, fock_env,
        amps_active, amps_env,
        left_active, right_active, intersect_active, left_env, right_env, intersect_env,
    )
    new_active = finish(
        total_a, amps_active, rank_active, gap_active, energy_active, aux_place * rows_a
    )
    new_env = finish(
        total_e[:, :rows_e, :wide_e], amps_env, rank_env, gap_env, energy_env, aux_place * rows_e
    )
    return (new_active, new_env)


def solution(mesh):
    ints, amps = P("pair", None, "aux"), P("pair", "aux", None)
    one, two, four = P("pair"), P("pair", None), P("pair", None, None, None)
    level = (ints, ints, amps, one, one, two, four, two, two)
    return jax.shard_map(
        functools.partial(shards, mesh.shape["pair"], mesh.shape["aux"]),
        mesh=mesh,
        in_specs=level + level,
        out_specs=(amps, amps),
        check_vma=False,
    )
```

profile of v0, /device:TPU:1, one launch (start us, length us, event | category | flops | bytes accessed | tf_op | source)
XLA Modules:
  0.0 49.9 jit_solution(9327510658484268985)
XLA Ops:
  0.6 0.8 %constant_dynamic-slice_fusion.1 = f32[10,8]{1,0:T(8,128)S(1)} fusion(f32[10,128]{1,0:T(8,128)} %param.23, s32[]{:T(128)S(6)} %select_n.14), kind=kLoop, calls=%fused_computation.8 | loop fusion | bytes 644 | tf_op jit(solution)/shard_map/dynamic_slice | solution.py:27
  1.4 0.7 %broadcast_compare_fusion = pred[10,8]{1,0:T(8,128)(4,1)S(1)} fusion(s32[8]{0:T(128)S(1)} %iota_add_fusion.1, s32[10]{0:T(128)} %rank_a.1), kind=kLoop, calls=%fused_computation.3 | loop fusion | flops 80 | bytes 152 | tf_op jit(solution)/shard_map/lt | solution.py:19
  2.1 1.4 %copy.20.nbr_a = s32[10,4]{1,0:T(8,128)} copy(s32[10,4]{0,1:T(4,128)} %param.26) | data formatting | bytes 320 | tf_op args[8]
  3.5 1.4 %copy.21.fock_a = f32[10,4]{1,0:T(8,128)} copy(f32[10,4]{0,1:T(4,128)} %param.25) | data formatting | bytes 320 | tf_op args[7]
  4.9 1.3 %copy.22.amps_e = bf16[4,3,48]{2,1,0:T(4,128)(2,1)} copy(bf16[4,3,48]{2,0,1:T(4,128)(2,1)} %param.29) | data formatting | bytes 2304 | tf_op args[11]
  6.1 0.0 copy-start.4
  6.1 0.0 copy-start
  6.1 0.0 copy-start.1
  6.1 0.0 copy-start.6
  6.2 0.0 copy-start.3
  6.2 0.0 copy-start.5
  6.2 0.0 copy-start.2
  6.2 0.0 copy-start.7
  6.2 40.5 %shard_map.185 = (f32[10,8,128]{2,1,0:T(8,128)}, f32[4,8,128]{2,1,0:T(8,128)}) custom-call(s32[10,4]{1,0:T(8,128)} %copy.20.nbr_a, s32[10]{0:T(128)} %rank_a.1, f32[10,4]{1,0:T(8,128)} %copy.21.fock_a, s32[4,4]{1,0:T(4,128)} %nbr_e.1, s32[4]{0:T(128)} %rank_e.1, f32[4,4]{1,0:T(4,128)} %fock_e.1, bf16[10,8,128]{2,1,0:T(8,128)(2,1)} %amps_a.1, ...), custom_call_target="tpu_custom_call" | custom-call | tf_op jit(solution)/shard_map/pallas_call | solution.py:277
  46.7 0.0 copy-done.4
  46.7 0.1 iota_compare_fusion
  46.8 0.0 copy-done
  46.8 0.0 copy-done.1
  46.8 0.0 copy-done.6
  46.8 1.5 %subtract_select_fusion = f32[10,8,128]{2,1,0:T(8,128)} fusion(f32[10,8,128]{2,1,0:T(8,128)} %get-tuple-element.4, bf16[10,8,128]{2,1,0:T(8,128)(2,1)S(1)} %copy-done, f32[10]{0:T(128)S(1)} %copy-done.6, f32[10,128]{1,0:T(8,128)S(1)} %copy-done.1, f32[10,8]{1,0:T(8,128)S(1)} %constant_dynamic-slice_fusion.1, pred[10,128]{1,0:T(8,128)(4,1)S(1)} %iota_compare_fusion, ...), kind=kLoop, calls=%fused_computation | loop fusion | flops 71680 | bytes 109240 | tf_op jit(solution)/shard_map/jit(_where)/select_n | solution.py:29
  48.3 0.0 copy-done.3
  48.3 0.1 constant_dynamic-slice_fusion
  48.4 0.0 copy-done.5
  48.4 0.1 broadcast_compare_fusion.1
  48.5 0.1 iota_compare_fusion.1
  48.5 0.0 copy-done.2
  48.5 0.0 copy-done.7
  48.5 0.8 %subtract_select_fusion.1 = f32[4,3,48]{2,1,0:T(4,128)S(1)} fusion(f32[4,8,128]{2,1,0:T(8,128)} %get-tuple-element.5, f32[4]{0:T(128)S(1)} %copy-done.7, f32[4,48]{1,0:T(4,128)S(1)} %copy-done.3, f32[4,3]{1,0:T(4,128)S(1)} %constant_dynamic-slice_fusion, pred[4,48]{1,0:T(4,128)(4,1)S(1)} %iota_compare_fusion.1, pred[4,3]{1,0:T(4,128)(4,1)S(1)} %broadcast_compare_fusion.1, ...), kind=kLoop, calls=%fused_computation.1 | loop fusion | flops 4032 | bytes 6796 | tf_op jit(solution)/shard_map/jit(_where)/select_n | solution.py:29
  49.3 0.6 %copy.24 = f32[4,3,48]{2,0,1:T(4,128)} copy(f32[4,3,48]{2,1,0:T(4,128)S(1)} %subtract_select_fusion.1) | data formatting | bytes 4608
  (2 shorter events, 0.0 us)
Async XLA Ops:
  6.1 40.6 %copy-start.4 = (s32[10]{0:T(128)S(1)}, s32[10]{0:T(128)}, u32[]{:S(2)}) copy-start(s32[10]{0:T(128)} %rank_a.1) | copy-start | bytes 124
  6.1 40.6 %copy-start = (bf16[10,8,128]{2,1,0:T(8,128)(2,1)S(1)}, bf16[10,8,128]{2,1,0:T(8,128)(2,1)}, u32[]{:S(2)}) copy-start(bf16[10,8,128]{2,1,0:T(8,128)(2,1)} %amps_a.1) | copy-start | bytes 61444
  6.1 40.6 %copy-start.1 = (f32[10,128]{1,0:T(8,128)S(1)}, f32[10,128]{1,0:T(8,128)}, u32[]{:S(2)}) copy-start(f32[10,128]{1,0:T(8,128)} %param.23) | copy-start | bytes 15364
  6.1 40.7 %copy-start.6 = (f32[10]{0:T(128)S(1)}, f32[10]{0:T(128)}, u32[]{:S(2)}) copy-start(f32[10]{0:T(128)} %param.22) | copy-start | bytes 124
  6.2 42.2 %copy-start.3 = (f32[4,48]{1,0:T(4,128)S(1)}, f32[4,48]{1,0:T(4,128)}, u32[]{:S(2)}) copy-start(f32[4,48]{1,0:T(4,128)} %param.32) | copy-start | bytes 2308
  6.2 42.2 %copy-start.5 = (s32[4]{0:T(128)S(1)}, s32[4]{0:T(128)}, u32[]{:S(2)}) copy-start(s32[4]{0:T(128)} %rank_e.1) | copy-start | bytes 52
  6.2 42.4 %copy-start.2 = (bf16[4,3,48]{2,0,1:T(4,128)(2,1)S(1)}, bf16[4,3,48]{2,0,1:T(4,128)(2,1)}, u32[]{:S(2)}) copy-start(bf16[4,3,48]{2,0,1:T(4,128)(2,1)} %param.29) | copy-start | bytes 3460
  6.2 42.3 %copy-start.7 = (f32[4]{0:T(128)S(1)}, f32[4]{0:T(128)}, u32[]{:S(2)}) copy-start(f32[4]{0:T(128)} %param.31) | copy-start | bytes 52
where the time goes:
time: 50.4 us; the launch traced here: 49.9 us
  Pallas kernels  40.5 us (80%)
  local copies, waits for them, and re-layouts  5.48 us (11%)
  other arithmetic  3.25 us (6%)
  between operations  0.71 us (1%)
    pallas_call x1, Pallas kernels, shards(): pl.pallas_call(functools.partial(kernel, npair, naux), out_shape=(jax.Sha...  40.5 us
    unnamed x20, local copies, waits for them, and re-layouts  4.63 us
    select_n x2, other arithmetic, finish(): jnp.where(inside, amp_shard.astype(F32) - summed / denominator, F32(0.0))  2.3 us

commit v1 on v0

v1 whole, which is shorter than its diff:
```python
import functools

import jax
import jax.numpy as jnp
from jax import lax
from jax.experimental import pallas as pl
from jax.experimental.pallas import tpu as pltpu
from jax.sharding import PartitionSpec as P

MESH = pl.DeviceIdType.MESH
F32, BF16, I32 = jnp.float32, jnp.bfloat16, jnp.int32
AHEAD = 4
CHUNKS = ((0, 5), (5, 10))


def halves(x):
    high = x.astype(BF16)
    return high, (x - high.astype(F32)).astype(BF16)


def dot(a, b, ca, cb):
    return lax.dot_general(a, b, (((ca,), (cb,)), ((), ())), preferred_element_type=F32)


def iota(shape, dim):
    return lax.broadcasted_iota(I32, shape, dim)


def cat(parts, axis):
    return jnp.concatenate(parts, axis=axis)


def hops(d, n):
    return min(d, n - d)


def kernel(
    npair, ny, nz,
    nbr_a, rank_a, fock_a, gap_a, nbr_e, rank_e, fock_e, gap_e,
    amps_a, en_a, amps_e, en_e,
    la_hbm, ra_hbm, sa_hbm, le_hbm, re_hbm, se_hbm,
    out_a, out_e,
    la, ra, sa, le, re, se,
    gat0, gat1, blk_a, blk_e, tot, bhl, wsel, amp_a, rec_a, amp_e, rec_e,
    send0, send1, recv0, recv1,
    la_sem, ra_sem, le_sem, re_sem, sa_sem, se_sem,
    gat_s, gat_r, blk_s, blk_r, ble_s, ble_r, rs_s, rs_r,
):
    me, grp = lax.axis_index("aux"), lax.axis_index("pair")
    naux = ny * nz
    my, mz = me // nz, lax.rem(me, nz)
    count_a, rows_a, wide_a = amps_a.shape
    rows_e, count_e, wide_e = amps_e.shape
    nb = nbr_a.shape[0]
    lanes = wide_a
    start_a, start_e = me * rows_a, me * rows_e
    gats, sends, recvs = (gat0, gat1), (send0, send1), (recv0, recv1)

    far = sorted(
        ((dy, dz) for dy in range(ny) for dz in range(nz) if dy or dz),
        key=lambda o: -(hops(o[0], ny) + hops(o[1], nz)),
    )

    def peer_of(o):
        return lax.rem(my + o[0], ny) * nz + lax.rem(mz + o[1], nz)

    barrier = pltpu.get_barrier_semaphore()
    for o in far:
        pl.semaphore_signal(barrier, inc=1, device_id={"aux": peer_of(o)}, device_id_type=MESH)
    for d in range(1, npair):
        pl.semaphore_signal(
            barrier, inc=1, device_id={"pair": lax.rem(grp + d, npair)}, device_id_type=MESH
        )

    def load_pair(p):
        return (
            pltpu.make_async_copy(la_hbm.at[p], la.at[p], la_sem.at[p]),
            pltpu.make_async_copy(ra_hbm.at[p], ra.at[p], ra_sem.at[p]),
        )

    load_env = (
        pltpu.make_async_copy(le_hbm, le, le_sem),
        pltpu.make_async_copy(re_hbm, re, re_sem),
    )
    load_se = pltpu.make_async_copy(se_hbm, se, se_sem)
    load_sa = pltpu.make_async_copy(sa_hbm, sa, sa_sem)
    for copy in (load_sa, load_se) + load_env:
        copy.start()
    for p in range(AHEAD):
        for copy in load_pair(p):
            copy.start()

    row8, col8 = iota((rows_a, lanes), 0), iota((rows_a, lanes), 1)
    for p in range(count_a):
        inside = (start_a + row8 < rank_a[p]) & (col8 < rank_a[p])
        own = jnp.where(inside, amps_a[p].astype(F32), 0.0)
        amp_a[p] = own
        own = own.astype(BF16)
        c = 0 if p < CHUNKS[0][1] else 1
        gats[c][me, p - CHUNKS[c][0]] = own
        blk_a[grp * count_a + p] = own

    def own_env(q):
        rows = jnp.zeros((8, wide_e), F32)
        r, s = iota((8, wide_e), 0), iota((8, wide_e), 1)
        for i in range(rows_e):
            rows = jnp.where(r == i, amps_e[i, q : q + 1, :].astype(F32), rows)
        inside = (r < rows_e) & (start_e + r < rank_e[q]) & (s < rank_e[q])
        return jnp.where(inside, rows, 0.0), inside

    owns = [own_env(q) for q in range(count_e)]
    for q in range(count_e):
        at = grp * count_e + q
        blk_e[at] = jnp.zeros(blk_e.shape[1:], BF16)
        blk_e[at, :, :wide_e] = owns[q][0].astype(BF16)

    pl.semaphore_wait(barrier, naux + npair - 2)

    def to_aux(c, o):
        e = o[0] * nz + o[1]
        slot = gats[c].at[me]
        return pltpu.make_async_remote_copy(
            src_ref=slot, dst_ref=slot, send_sem=gat_s.at[c, e], recv_sem=gat_r.at[c, e],
            device_id={"aux": peer_of(o)}, device_id_type=MESH,
        )

    def to_pair(d, block, count, s, r):
        slot = block.at[pl.ds(grp * count, count)]
        return pltpu.make_async_remote_copy(
            src_ref=slot, dst_ref=slot, send_sem=s.at[d], recv_sem=r.at[d],
            device_id={"pair": lax.rem(grp + d, npair)}, device_id_type=MESH,
        )

    for c in range(2):
        for o in far:
            to_aux(c, o).start()
        if c == 0:
            for d in range(1, npair):
                to_pair(d, blk_a, count_a, blk_s, blk_r).start()
                to_pair(d, blk_e, count_e, ble_s, ble_r).start()

    for p in range(count_a):
        inside = (start_a + row8 < rank_a[p]) & (col8 < rank_a[p])
        across = jnp.broadcast_to(en_a[p : p + 1, :], (rows_a, lanes))
        down = jnp.sum(jnp.where(col8 == start_a + row8, across, 0.0), axis=1, keepdims=True)
        rec_a[p] = jnp.where(inside, 1.0 / (across + down + gap_a[p]), 0.0)
    r48, c48 = iota((8, wide_e), 0), iota((8, wide_e), 1)
    for q in range(count_e):
        across = jnp.broadcast_to(en_e[q : q + 1, :], (8, wide_e))
        down = jnp.sum(jnp.where(c48 == start_e + r48, across, 0.0), axis=1, keepdims=True)
        denom = jnp.where(r48 < rows_e, across + down + gap_e[q], 1.0)
        rec_e[q] = jnp.where(owns[q][1], 1.0 / denom, 0.0)
        amp_e[q] = owns[q][0]

    load_sa.wait()
    k_in, k_out = iota((nb * wide_a, lanes), 0), iota((nb * wide_a, lanes), 1)
    group = nb * rows_a
    k_at = lax.rem(k_out, group)
    source = (k_at // rows_a) * wide_a + start_a + lax.rem(k_at, rows_a)
    pick = jnp.where((k_in == source) & (k_out < 2 * group), 1.0, 0.0).astype(BF16)

    def overs(p):
        return cat([sa[p, k] for k in range(nb)], 1)

    @pl.loop(0, count_a)
    def _(p):
        wsel[p] = dot(overs(p), pick, 1, 0).astype(BF16)

    for copy in load_env:
        copy.wait()
    le_all = le[...].reshape(count_e * wide_e, le.shape[2])
    pad = 64 - wide_e
    gap_rows = jnp.zeros((pad, re.shape[2]), BF16)
    re_all = cat([x for q in range(count_e) for x in (re[q], gap_rows)], 0)
    base_e = dot(le_all, re_all, 1, 1)
    low_lanes = iota((wide_e, lanes), 1) < 64
    base_h = []
    for h in range(count_e // 2):
        block = base_e[:, h * lanes : (h + 1) * lanes]
        a, b = 2 * h * wide_e, (2 * h + 1) * wide_e
        base_h.append(jnp.where(low_lanes, block[a : a + wide_e], block[b : b + wide_e]))

    @pl.loop(0, count_a)
    def _(p):
        @pl.when(p + AHEAD < count_a)
        def _():
            for copy in load_pair(p + AHEAD):
                copy.start()

        for copy in load_pair(p):
            copy.wait()
        base = dot(la[p], ra[p], 1, 1)
        tot[p] = base
        bhl[p] = cat(halves(base), 0)

    @pl.loop(1, npair)
    def _(d):
        to_pair(d, blk_a, count_a, blk_s, blk_r).wait()
        to_pair(d, blk_e, count_e, ble_s, ble_r).wait()

    load_se.wait()
    fill = jnp.zeros((pad, wide_e), BF16)
    lane16, row16 = iota((16, lanes), 1), iota((16, lanes), 0)
    keep16 = (lane16 < 64) == (row16 < 8)
    pin, pout = iota((wide_e, lanes), 0), iota((wide_e, lanes), 1)
    pat = lax.rem(pout, 64)
    inner = lax.rem(pat, 8)
    sums = []
    for h in range(count_e // 2):
        q0, q1 = 2 * h, 2 * h + 1
        parts, chosen = [], jnp.zeros((wide_e, lanes), F32)
        for k in range(nb):
            both = cat([se[q0, k], fill, se[q1, k], fill], 0)
            rows = cat(
                [blk_e[nbr_e[q, k], :, :wide_e].astype(F32) for q in (q0, q1)], 0
            ).astype(BF16)
            prod = dot(rows, both, 1, 1)
            scale = jnp.where(row16 < 8, fock_e[q0, k], fock_e[q1, k])
            parts.append(jnp.where(keep16, prod * scale, 0.0))
            for b, q in enumerate((q0, q1)):
                sel = jnp.where(
                    (pin == start_e + inner) & (inner < rows_e) & (pat // 8 == 2 * k + b), 1.0, 0.0
                ).astype(BF16)
                chosen = chosen + dot(se[q, k], sel, 1, 0)
        near = cat(halves(cat(parts, 0)), 0)
        sums.append((base_h[h] + dot(chosen.astype(BF16), near, 1, 0)).astype(BF16))
    both_e = cat(sums, 0)
    srow, scol = iota((lanes, 2 * wide_e), 0), iota((lanes, 2 * wide_e), 1)
    sj, sr = srow // 8, lax.rem(srow, 8)
    si = lax.rem(sr, 4)
    spread = jnp.where(
        (scol == (sr // 4) * wide_e + rows_e * sj + si) & (si < rows_e), 1.0, 0.0
    ).astype(BF16)
    packed = dot(spread, both_e, 1, 0)
    for j in range(naux):
        send1[j, CHUNKS[1][1] - CHUNKS[1][0]] = packed[8 * j : 8 * j + 8].astype(BF16)

    @pl.loop(0, count_a)
    def _(p):
        rows = []
        zero = jnp.zeros((rows_a, wide_a), F32)
        for k in range(nb):
            near = blk_a[nbr_a[k, p]].astype(F32)
            rows.append(cat([near if i == k else zero for i in range(nb)], 1))
        right = dot(cat(rows, 0).astype(BF16), overs(p), 1, 1)
        right = cat(
            [right[k * rows_a : (k + 1) * rows_a] * fock_a[k, p] for k in range(nb)], 0
        )
        tot[p] = tot[p] + dot(wsel[p][:, : 2 * group], cat(halves(right), 0), 1, 0)

    def sums_to(c, o):
        e = o[0] * nz + o[1]
        return pltpu.make_async_remote_copy(
            src_ref=sends[c].at[peer_of(o)], dst_ref=recvs[c].at[e],
            send_sem=rs_s.at[c, e], recv_sem=rs_r.at[c, e],
            device_id={"aux": peer_of(o)}, device_id_type=MESH,
        )

    for c, (lo, hi) in enumerate(CHUNKS):
        for o in far:
            to_aux(c, o).wait()
        for p in range(lo, hi):
            amp = gats[c][:, p - lo].astype(F32).reshape(wide_a, wide_a).astype(BF16)
            x = dot(cat([amp, amp], 0), bhl[p], 0, 0)
            y = dot(cat(halves(x), 1), cat([amp, amp], 1), 1, 1)
            total = (tot[p] + x + y).reshape(naux, rows_a, wide_a)
            sends[c][:, p - lo] = total.astype(BF16)
        for o in far:
            sums_to(c, o).start()

    near_first = far[::-1]
    for c, (lo, hi) in enumerate(CHUNKS):
        acc = sends[c][me].astype(F32)
        for o in near_first:
            sums_to(c, o).wait()
            acc = acc + recvs[c][o[0] * nz + o[1]].astype(F32)
        for p in range(lo, hi):
            out_a[p] = amp_a[p] - acc[p - lo] * rec_a[p]
        if c == 1:
            env = acc[hi - lo]
            turned = pltpu.roll(env, 64, 1)
            for q in range(count_e):
                r = 4 * (q // 2)
                block = (env if q % 2 == 0 else turned)[r : r + 4, :wide_e]
                new = amp_e[q][:4] - block * rec_e[q][:4]
                for i in range(rows_e):
                    out_e[i, q : q + 1, :] = new[i : i + 1]


def shards(
    npair, ny, nz,
    left_active, right_active, amps_active, rank_active, gap_active, energy_active,
    intersect_active, fock_active, neighbor_active,
    left_env, right_env, amps_env, rank_env, gap_env, energy_env,
    intersect_env, fock_env, neighbor_env,
):
    naux = ny * nz
    count_a, rows_a, wide_a = amps_active.shape
    count_e, rows_e, wide_e = amps_env.shape
    nb = neighbor_active.shape[1]
    smem = pl.BlockSpec(memory_space=pltpu.SMEM)
    vmem = pl.BlockSpec(memory_space=pltpu.VMEM)
    anyw = pl.BlockSpec(memory_space=pl.ANY)
    dma = pltpu.SemaphoreType.DMA
    n0 = CHUNKS[0][1] - CHUNKS[0][0]
    n1 = CHUNKS[1][1] - CHUNKS[1][0]
    new_active, new_env = pl.pallas_call(
        functools.partial(kernel, npair, ny, nz),
        out_shape=(
            jax.ShapeDtypeStruct((count_a, rows_a, wide_a), F32),
            jax.ShapeDtypeStruct((rows_e, count_e, wide_e), F32),
        ),
        in_specs=[smem] * 8 + [vmem] * 4 + [anyw] * 6,
        out_specs=(vmem, vmem),
        scratch_shapes=[
            pltpu.VMEM(left_active.shape, BF16),
            pltpu.VMEM(right_active.shape, BF16),
            pltpu.VMEM(intersect_active.shape, BF16),
            pltpu.VMEM(left_env.shape, BF16),
            pltpu.VMEM(right_env.shape, BF16),
            pltpu.VMEM(intersect_env.shape, BF16),
            pltpu.VMEM((naux, n0, rows_a, wide_a), BF16),
            pltpu.VMEM((naux, n1, rows_a, wide_a), BF16),
            pltpu.VMEM((npair * count_a, rows_a, wide_a), BF16),
            pltpu.VMEM((npair * count_e, 8, 128), BF16),
            pltpu.VMEM((count_a, wide_a, wide_a), F32),
            pltpu.VMEM((count_a, 2 * wide_a, wide_a), BF16),
            pltpu.VMEM((count_a, wide_a, 128), BF16),
            pltpu.VMEM((count_a, rows_a, wide_a), F32),
            pltpu.VMEM((count_a, rows_a, wide_a), F32),
            pltpu.VMEM((count_e, 8, wide_e), F32),
            pltpu.VMEM((count_e, 8, wide_e), F32),
            pltpu.VMEM((naux, n0, rows_a, wide_a), BF16),
            pltpu.VMEM((naux, n1 + 1, rows_a, wide_a), BF16),
            pltpu.VMEM((naux, n0, rows_a, wide_a), BF16),
            pltpu.VMEM((naux, n1 + 1, rows_a, wide_a), BF16),
            dma((count_a,)), dma((count_a,)), dma, dma, dma, dma,
            dma((2, naux)), dma((2, naux)),
            dma((npair,)), dma((npair,)), dma((npair,)), dma((npair,)),
            dma((2, naux)), dma((2, naux)),
        ],
        compiler_params=pltpu.CompilerParams(
            collective_id=0, has_side_effects=True, vmem_limit_bytes=60 * 1024 * 1024
        ),
    )(
        neighbor_active.T, rank_active, fock_active.T, gap_active,
        neighbor_env, rank_env, fock_env, gap_env,
        amps_active, energy_active, amps_env.transpose(1, 0, 2), energy_env,
        left_active, right_active, intersect_active, left_env, right_env, intersect_env,
    )
    return new_active, new_env.transpose(1, 0, 2)


def solution(mesh):
    ints, amps = P("pair", None, "aux"), P("pair", "aux", None)
    one, two, four = P("pair"), P("pair", None), P("pair", None, None, None)
    level = (ints, ints, amps, one, one, two, four, two, two)
    naux = mesh.shape["aux"]
    ny = next(n for n in range(int(naux**0.5), 0, -1) if naux % n == 0)
    return jax.shard_map(
        functools.partial(shards, mesh.shape["pair"], ny, naux // ny),
        mesh=mesh,
        in_specs=level + level,
        out_specs=(amps, amps),
        check_vma=False,
    )
```

time: 50.4 us -> 33.2 us (0.66)
  the two profiles are of different devices: /device:TPU:1 before, /device:TPU:0 now
where the time goes in v1:
time: 33.2 us; the launch traced here: 32.9 us
  Pallas kernels  29.6 us (89%)
  local copies, waits for them, and re-layouts  2.68 us (8%)
  between operations  0.65 us (2%)
    pallas_call x1, Pallas kernels, shards(): pl.pallas_call(functools.partial(kernel, npair, ny, nz), out_shape=(jax.S...  29.6 us
    unnamed x2, local copies, waits for them, and re-layouts  2.68 us

profile of v1, /device:TPU:0, one launch (start us, length us, event | category | flops | bytes accessed | tf_op | source)
XLA Modules:
  0.0 32.9 jit_solution(17875619271402535261)
XLA Ops:
  0.6 29.6 %shard_map.185 = (f32[10,8,128]{2,1,0:T(8,128)}, f32[3,4,48]{2,1,0:T(4,128)}) custom-call(s32[4,10]{1,0:T(4,128)} %bitcast.6, s32[10]{0:T(128)} %rank_a.1, f32[4,10]{1,0:T(4,128)} %bitcast.7, f32[10]{0:T(128)} %gap_a.1, s32[4,4]{1,0:T(4,128)} %nbr_e.1, s32[4]{0:T(128)} %rank_e.1, f32[4,4]{1,0:T(4,128)} %fock_e.1, f32[4]{0:T(128)} %gap_e.1, ...), custom_call_target="tpu_custom_call" | custom-call | tf_op jit(solution)/shard_map/pallas_call | solution.py:307
  30.2 1.4 %copy.22 = f32[10,8,128]{2,1,0:T(8,128)} copy(f32[10,8,128]{2,1,0:T(8,128)} %get-tuple-element.8) | data formatting | bytes 81920
  31.6 1.3 %copy.23 = f32[4,3,48]{2,0,1:T(4,128)} copy(f32[4,3,48]{2,0,1:T(4,128)} %bitcast.4) | data formatting | bytes 4608

commit v2 on v1

--- a/solution.py
+++ b/solution.py
@@ -9,7 +9,8 @@
 
 MESH = pl.DeviceIdType.MESH
 F32, BF16, I32 = jnp.float32, jnp.bfloat16, jnp.int32
-AHEAD = 4
+FIRST, DEPTH = 2, 3
+VMEM = 36 * 1024 * 1024
 CHUNKS = ((0, 5), (5, 10))
 
 
@@ -36,16 +37,25 @@
 
 def kernel(
     npair, ny, nz,
-    nbr_a, rank_a, fock_a, gap_a, nbr_e, rank_e, fock_e, gap_e,
-    amps_a, en_a, amps_e, en_e,
+    *refs,
+):
+    small_hbm, refs = refs[:12], refs[12:]
+    small, refs = refs[8 : 8 + 12], refs[:8] + refs[8 + 12 :]
+    body(npair, ny, nz, small_hbm, small, *refs)
+
+
+def body(
+    npair, ny, nz, small_hbm, small,
     la_hbm, ra_hbm, sa_hbm, le_hbm, re_hbm, se_hbm,
     out_a, out_e,
     la, ra, sa, le, re, se,
-    gat0, gat1, blk_a, blk_e, tot, bhl, wsel, amp_a, rec_a, amp_e, rec_e,
+    gat, blk_a, blk_e, tot, cpl, bhl, wsel, wsel_e, amp_a, rec_a, amp_e, rec_e,
     send0, send1, recv0, recv1,
-    la_sem, ra_sem, le_sem, re_sem, sa_sem, se_sem,
+    small_sem, la_sem, ra_sem, le_sem, re_sem, sa_sem, se_sem,
     gat_s, gat_r, blk_s, blk_r, ble_s, ble_r, rs_s, rs_r,
 ):
+    nbr_a, rank_a, fock_a, gap_a, nbr_e, rank_e, fock_e, gap_e = small[:8]
+    amps_a, en_a, amps_e, en_e = small[8:]
     me, grp = lax.axis_index("aux"), lax.axis_index("pair")
     naux = ny * nz
     my, mz = me // nz, lax.rem(me, nz)
@@ -54,7 +64,7 @@
     nb = nbr_a.shape[0]
     lanes = wide_a
     start_a, start_e = me * rows_a, me * rows_e
-    gats, sends, recvs = (gat0, gat1), (send0, send1), (recv0, recv1)
+    sends, recvs = (send0, send1), (recv0, recv1)
 
     far = sorted(
         ((dy, dz) for dy in range(ny) for dz in range(nz) if dy or dz),
@@ -84,11 +94,25 @@
     )
     load_se = pltpu.make_async_copy(se_hbm, se, se_sem)
     load_sa = pltpu.make_async_copy(sa_hbm, sa, sa_sem)
-    for copy in (load_sa, load_se) + load_env:
+    load_small = [
+        pltpu.make_async_copy(src, dst, small_sem.at[i])
+        for i, (src, dst) in enumerate(zip(small_hbm, small))
+    ]
+    for copy in load_small:
         copy.start()
-    for p in range(AHEAD):
+    load_sa.start()
+    load_se.start()
+    for copy in load_env:
+        copy.start()
+
+    def start_pair(p):
         for copy in load_pair(p):
             copy.start()
+
+    for p in range(FIRST):
+        start_pair(p)
+    for copy in load_small:
+        copy.wait()
 
     row8, col8 = iota((rows_a, lanes), 0), iota((rows_a, lanes), 1)
     for p in range(count_a):
@@ -96,8 +120,7 @@
         own = jnp.where(inside, amps_a[p].astype(F32), 0.0)
         amp_a[p] = own
         own = own.astype(BF16)
-        c = 0 if p < CHUNKS[0][1] else 1
-        gats[c][me, p - CHUNKS[c][0]] = own
+        gat[me, p] = own
         blk_a[grp * count_a + p] = own
 
     def own_env(q):
@@ -116,11 +139,11 @@
 
     pl.semaphore_wait(barrier, naux + npair - 2)
 
-    def to_aux(c, o):
+    def to_aux(o):
         e = o[0] * nz + o[1]
-        slot = gats[c].at[me]
+        slot = gat.at[me]
         return pltpu.make_async_remote_copy(
-            src_ref=slot, dst_ref=slot, send_sem=gat_s.at[c, e], recv_sem=gat_r.at[c, e],
+            src_ref=slot, dst_ref=slot, send_sem=gat_s.at[e], recv_sem=gat_r.at[e],
             device_id={"aux": peer_of(o)}, device_id_type=MESH,
         )
 
@@ -131,13 +154,14 @@
             device_id={"pair": lax.rem(grp + d, npair)}, device_id_type=MESH,
         )
 
-    for c in range(2):
-        for o in far:
-            to_aux(c, o).start()
-        if c == 0:
-            for d in range(1, npair):
-                to_pair(d, blk_a, count_a, blk_s, blk_r).start()
-                to_pair(d, blk_e, count_e, ble_s, ble_r).start()
+    for d in range(1, npair):
+        to_pair(d, blk_a, count_a, blk_s, blk_r).start()
+        to_pair(d, blk_e, count_e, ble_s, ble_r).start()
+    for o in far:
+        to_aux(o).start()
+
+    for p in range(FIRST, DEPTH):
+        start_pair(p)
 
     for p in range(count_a):
         inside = (start_a + row8 < rank_a[p]) & (col8 < rank_a[p])
@@ -153,8 +177,9 @@
         amp_e[q] = owns[q][0]
 
     load_sa.wait()
+    load_se.wait()
+    group = nb * rows_a
     k_in, k_out = iota((nb * wide_a, lanes), 0), iota((nb * wide_a, lanes), 1)
-    group = nb * rows_a
     k_at = lax.rem(k_out, group)
     source = (k_at // rows_a) * wide_a + start_a + lax.rem(k_at, rows_a)
     pick = jnp.where((k_in == source) & (k_out < 2 * group), 1.0, 0.0).astype(BF16)
@@ -162,9 +187,21 @@
     def overs(p):
         return cat([sa[p, k] for k in range(nb)], 1)
 
-    @pl.loop(0, count_a)
-    def _(p):
+    for p in range(count_a):
         wsel[p] = dot(overs(p), pick, 1, 0).astype(BF16)
+
+    pin, pout = iota((wide_e, lanes), 0), iota((wide_e, lanes), 1)
+    pat = lax.rem(pout, 64)
+    inner = lax.rem(pat, 8)
+    for h in range(count_e // 2):
+        chosen = jnp.zeros((wide_e, lanes), F32)
+        for k in range(nb):
+            for b in range(2):
+                sel = jnp.where(
+                    (pin == start_e + inner) & (inner < rows_e) & (pat // 8 == 2 * k + b), 1.0, 0.0
+                ).astype(BF16)
+                chosen = chosen + dot(se[2 * h + b, k], sel, 1, 0)
+        wsel_e[h] = chosen.astype(BF16)
 
     for copy in load_env:
         copy.wait()
@@ -180,35 +217,42 @@
         a, b = 2 * h * wide_e, (2 * h + 1) * wide_e
         base_h.append(jnp.where(low_lanes, block[a : a + wide_e], block[b : b + wide_e]))
 
-    @pl.loop(0, count_a)
-    def _(p):
-        @pl.when(p + AHEAD < count_a)
-        def _():
-            for copy in load_pair(p + AHEAD):
-                copy.start()
-
+    def ladder(p):
+        if not isinstance(p, int):
+            start_pair(p + DEPTH)
         for copy in load_pair(p):
             copy.wait()
         base = dot(la[p], ra[p], 1, 1)
         tot[p] = base
         bhl[p] = cat(halves(base), 0)
 
-    @pl.loop(1, npair)
-    def _(d):
-        to_pair(d, blk_a, count_a, blk_s, blk_r).wait()
-        to_pair(d, blk_e, count_e, ble_s, ble_r).wait()
-
-    load_se.wait()
+    pl.loop(0, count_a - DEPTH)(ladder)
+    for p in range(count_a - DEPTH, count_a - 3):
+        ladder(p)
+
+    lane_k = iota((wide_a, 2 * group), 1)
+    at_k = lax.rem(lane_k, group) // rows_a
+    zero = jnp.zeros((rows_a, wide_a), F32)
+
+    def couple(p):
+        rows, scale = [], jnp.zeros((wide_a, 2 * group), F32)
+        for k in range(nb):
+            near = blk_a[nbr_a[k, p]].astype(F32)
+            rows.append(cat([near if i == k else zero for i in range(nb)], 1))
+            scale = jnp.where(at_k == k, fock_a[k, p], scale)
+        rows = cat(rows, 0).astype(BF16)
+        right = dot(overs(p), cat([rows, rows], 0), 1, 1) * scale
+        high = right.astype(BF16).astype(F32)
+        right = jnp.where(lane_k < group, high, right - high).astype(BF16)
+        cpl[p] = dot(wsel[p][:, : 2 * group], right, 1, 1)
+
     fill = jnp.zeros((pad, wide_e), BF16)
     lane16, row16 = iota((16, lanes), 1), iota((16, lanes), 0)
     keep16 = (lane16 < 64) == (row16 < 8)
-    pin, pout = iota((wide_e, lanes), 0), iota((wide_e, lanes), 1)
-    pat = lax.rem(pout, 64)
-    inner = lax.rem(pat, 8)
-    sums = []
-    for h in range(count_e // 2):
+
+    def couple_env(h):
         q0, q1 = 2 * h, 2 * h + 1
-        parts, chosen = [], jnp.zeros((wide_e, lanes), F32)
+        parts = []
         for k in range(nb):
             both = cat([se[q0, k], fill, se[q1, k], fill], 0)
             rows = cat(
@@ -217,14 +261,18 @@
             prod = dot(rows, both, 1, 1)
             scale = jnp.where(row16 < 8, fock_e[q0, k], fock_e[q1, k])
             parts.append(jnp.where(keep16, prod * scale, 0.0))
-            for b, q in enumerate((q0, q1)):
-                sel = jnp.where(
-                    (pin == start_e + inner) & (inner < rows_e) & (pat // 8 == 2 * k + b), 1.0, 0.0
-                ).astype(BF16)
-                chosen = chosen + dot(se[q, k], sel, 1, 0)
         near = cat(halves(cat(parts, 0)), 0)
-        sums.append((base_h[h] + dot(chosen.astype(BF16), near, 1, 0)).astype(BF16))
-    both_e = cat(sums, 0)
+        return (base_h[h] + dot(wsel_e[h], near, 1, 0)).astype(BF16)
+
+    @pl.loop(1, npair)
+    def _(d):
+        to_pair(d, blk_a, count_a, blk_s, blk_r).wait()
+        to_pair(d, blk_e, count_e, ble_s, ble_r).wait()
+
+    for p in range(count_a // 2):
+        couple(p)
+    ladder(7)
+    both_e = cat([couple_env(h) for h in range(count_e // 2)], 0)
     srow, scol = iota((lanes, 2 * wide_e), 0), iota((lanes, 2 * wide_e), 1)
     sj, sr = srow // 8, lax.rem(srow, 8)
     si = lax.rem(sr, 4)
@@ -234,19 +282,10 @@
     packed = dot(spread, both_e, 1, 0)
     for j in range(naux):
         send1[j, CHUNKS[1][1] - CHUNKS[1][0]] = packed[8 * j : 8 * j + 8].astype(BF16)
-
-    @pl.loop(0, count_a)
-    def _(p):
-        rows = []
-        zero = jnp.zeros((rows_a, wide_a), F32)
-        for k in range(nb):
-            near = blk_a[nbr_a[k, p]].astype(F32)
-            rows.append(cat([near if i == k else zero for i in range(nb)], 1))
-        right = dot(cat(rows, 0).astype(BF16), overs(p), 1, 1)
-        right = cat(
-            [right[k * rows_a : (k + 1) * rows_a] * fock_a[k, p] for k in range(nb)], 0
-        )
-        tot[p] = tot[p] + dot(wsel[p][:, : 2 * group], cat(halves(right), 0), 1, 0)
+    ladder(8)
+    for p in range(count_a // 2, count_a):
+        couple(p)
+    ladder(9)
 
     def sums_to(c, o):
         e = o[0] * nz + o[1]
@@ -257,13 +296,14 @@
         )
 
     for c, (lo, hi) in enumerate(CHUNKS):
-        for o in far:
-            to_aux(c, o).wait()
+        if c == 0:
+            for o in far:
+                to_aux(o).wait()
         for p in range(lo, hi):
-            amp = gats[c][:, p - lo].astype(F32).reshape(wide_a, wide_a).astype(BF16)
+            amp = gat[:, p].astype(F32).reshape(wide_a, wide_a).astype(BF16)
             x = dot(cat([amp, amp], 0), bhl[p], 0, 0)
             y = dot(cat(halves(x), 1), cat([amp, amp], 1), 1, 1)
-            total = (tot[p] + x + y).reshape(naux, rows_a, wide_a)
+            total = (tot[p] + cpl[p] + x + y).reshape(naux, rows_a, wide_a)
             sends[c][:, p - lo] = total.astype(BF16)
         for o in far:
             sums_to(c, o).start()
@@ -298,34 +338,41 @@
     count_a, rows_a, wide_a = amps_active.shape
     count_e, rows_e, wide_e = amps_env.shape
     nb = neighbor_active.shape[1]
-    smem = pl.BlockSpec(memory_space=pltpu.SMEM)
     vmem = pl.BlockSpec(memory_space=pltpu.VMEM)
-    anyw = pl.BlockSpec(memory_space=pl.ANY)
+    hbm = pl.BlockSpec(memory_space=pltpu.HBM)
     dma = pltpu.SemaphoreType.DMA
     n0 = CHUNKS[0][1] - CHUNKS[0][0]
     n1 = CHUNKS[1][1] - CHUNKS[1][0]
+    small = (
+        neighbor_active.T, rank_active, fock_active.T, gap_active,
+        neighbor_env, rank_env, fock_env, gap_env,
+        amps_active, energy_active, amps_env.transpose(1, 0, 2), energy_env,
+    )
     new_active, new_env = pl.pallas_call(
         functools.partial(kernel, npair, ny, nz),
         out_shape=(
             jax.ShapeDtypeStruct((count_a, rows_a, wide_a), F32),
             jax.ShapeDtypeStruct((rows_e, count_e, wide_e), F32),
         ),
-        in_specs=[smem] * 8 + [vmem] * 4 + [anyw] * 6,
+        in_specs=[hbm] * 18,
         out_specs=(vmem, vmem),
-        scratch_shapes=[
+        scratch_shapes=[pltpu.SMEM(x.shape, x.dtype) for x in small[:8]]
+        + [pltpu.VMEM(x.shape, x.dtype) for x in small[8:]]
+        + [
             pltpu.VMEM(left_active.shape, BF16),
             pltpu.VMEM(right_active.shape, BF16),
             pltpu.VMEM(intersect_active.shape, BF16),
             pltpu.VMEM(left_env.shape, BF16),
             pltpu.VMEM(right_env.shape, BF16),
             pltpu.VMEM(intersect_env.shape, BF16),
-            pltpu.VMEM((naux, n0, rows_a, wide_a), BF16),
-            pltpu.VMEM((naux, n1, rows_a, wide_a), BF16),
+            pltpu.VMEM((naux, count_a, rows_a, wide_a), BF16),
             pltpu.VMEM((npair * count_a, rows_a, wide_a), BF16),
             pltpu.VMEM((npair * count_e, 8, 128), BF16),
             pltpu.VMEM((count_a, wide_a, wide_a), F32),
+            pltpu.VMEM((count_a, wide_a, wide_a), F32),
             pltpu.VMEM((count_a, 2 * wide_a, wide_a), BF16),
             pltpu.VMEM((count_a, wide_a, 128), BF16),
+            pltpu.VMEM((count_e // 2, wide_e, 128), BF16),
             pltpu.VMEM((count_a, rows_a, wide_a), F32),
             pltpu.VMEM((count_a, rows_a, wide_a), F32),
             pltpu.VMEM((count_e, 8, wide_e), F32),
@@ -334,19 +381,20 @@
             pltpu.VMEM((naux, n1 + 1, rows_a, wide_a), BF16),
             pltpu.VMEM((naux, n0, rows_a, wide_a), BF16),
             pltpu.VMEM((naux, n1 + 1, rows_a, wide_a), BF16),
-            dma((count_a,)), dma((count_a,)), dma, dma, dma, dma,
-            dma((2, naux)), dma((2, naux)),
+            dma((12,)), dma((count_a,)), dma((count_a,)), dma, dma, dma, dma,
+            dma((naux,)), dma((naux,)),
             dma((npair,)), dma((npair,)), dma((npair,)), dma((npair,)),
             dma((2, naux)), dma((2, naux)),
         ],
         compiler_params=pltpu.CompilerParams(
-            collective_id=0, has_side_effects=True, vmem_limit_bytes=60 * 1024 * 1024
+            collective_id=0, has_side_effects=True, vmem_limit_bytes=VMEM
         ),
     )(
-        neighbor_active.T, rank_active, fock_active.T, gap_active,
-        neighbor_env, rank_env, fock_env, gap_env,
-        amps_active, energy_active, amps_env.transpose(1, 0, 2), energy_env,
-        left_active, right_active, intersect_active, left_env, right_env, intersect_env,
+        *(
+            pltpu.with_memory_space_constraint(x, pltpu.HBM)
+            for x in small
+            + (left_active, right_active, intersect_active, left_env, right_env, intersect_env)
+        )
     )
     return new_active, new_env.transpose(1, 0, 2)
 

time: 33.2 us -> 28.1 us (0.85)
  Pallas kernels: 29.6 us -> 26.1 us
  local copies, waits for them, and re-layouts: 2.68 us -> 1.21 us
    pallas_call x1, Pallas kernels: 29.6 us -> 26.1 us  [shards(): pl.pallas_call(functools.partial(kernel, npair, ny, nz), out_shape=(jax.S...]
    unnamed x2, local copies, waits for them, and re-layouts: 2.68 us -> 1.21 us
where the time goes in v2:
time: 28.1 us; the launch traced here: 28 us
  Pallas kernels  26.1 us (93%)
  local copies, waits for them, and re-layouts  1.21 us (4%)
  between operations  0.65 us (2%)
    pallas_call x1, Pallas kernels, shards(): pl.pallas_call(functools.partial(kernel, npair, ny, nz), out_shape=(jax.S...  26.1 us
    unnamed x2, local copies, waits for them, and re-layouts  1.21 us

profile of v2, /device:TPU:0, one launch (start us, length us, event | category | flops | bytes accessed | tf_op | source)
XLA Modules:
  0.0 28.0 jit_solution(3378568947334231526)
XLA Ops:
  0.6 26.1 %shard_map.185 = (f32[10,8,128]{2,1,0:T(8,128)S(1)}, f32[3,4,48]{2,1,0:T(4,128)S(1)}) custom-call(s32[4,10]{1,0:T(4,128)} %bitcast.6, s32[10]{0:T(128)} %refs_1_.1, f32[4,10]{1,0:T(4,128)} %bitcast.7, f32[10]{0:T(128)} %refs_3_.1, s32[4,4]{1,0:T(4,128)} %refs_4_.1, s32[4]{0:T(128)} %refs_5_.1, f32[4,4]{1,0:T(4,128)} %refs_6_.1, f32[4]{0:T(128)} %refs_7_.1, ...), custom_call_target="tpu_custom_call" | custom-call | tf_op jit(solution)/shard_map/pallas_call | solution.py:351
  26.7 0.6 %copy.22 = f32[10,8,128]{2,1,0:T(8,128)} copy(f32[10,8,128]{2,1,0:T(8,128)S(1)} %get-tuple-element.8) | data formatting | bytes 81920
  27.4 0.6 %copy.23 = f32[4,3,48]{2,0,1:T(4,128)} copy(f32[4,3,48]{2,0,1:T(4,128)S(1)} %bitcast.4) | data formatting | bytes 4608

commit v3 on v2

--- a/solution.py
+++ b/solution.py
@@ -9,7 +9,7 @@
 
 MESH = pl.DeviceIdType.MESH
 F32, BF16, I32 = jnp.float32, jnp.bfloat16, jnp.int32
-FIRST, DEPTH = 2, 3
+FIRST, DEPTH = 2, 5
 VMEM = 36 * 1024 * 1024
 CHUNKS = ((0, 5), (5, 10))
 
@@ -49,7 +49,7 @@
     la_hbm, ra_hbm, sa_hbm, le_hbm, re_hbm, se_hbm,
     out_a, out_e,
     la, ra, sa, le, re, se,
-    gat, blk_a, blk_e, tot, cpl, bhl, wsel, wsel_e, amp_a, rec_a, amp_e, rec_e,
+    gat, blk_a, blk_e, tot, b16, near, wsel, wsel_e, amp_a, rec_a, amp_e, rec_e,
     send0, send1, recv0, recv1,
     small_sem, la_sem, ra_sem, le_sem, re_sem, sa_sem, se_sem,
     gat_s, gat_r, blk_s, blk_r, ble_s, ble_r, rs_s, rs_r,
@@ -140,17 +140,22 @@
     pl.semaphore_wait(barrier, naux + npair - 2)
 
     def to_aux(o):
-        e = o[0] * nz + o[1]
         slot = gat.at[me]
         return pltpu.make_async_remote_copy(
-            src_ref=slot, dst_ref=slot, send_sem=gat_s.at[e], recv_sem=gat_r.at[e],
+            src_ref=slot, dst_ref=slot, send_sem=gat_s, recv_sem=gat_r,
             device_id={"aux": peer_of(o)}, device_id_type=MESH,
         )
+
+    def arrived(ref, send, recv):
+        pltpu.make_async_remote_copy(
+            src_ref=ref, dst_ref=ref, send_sem=send, recv_sem=recv,
+            device_id={"aux": peer_of(far[0])}, device_id_type=MESH,
+        ).wait()
 
     def to_pair(d, block, count, s, r):
         slot = block.at[pl.ds(grp * count, count)]
         return pltpu.make_async_remote_copy(
-            src_ref=slot, dst_ref=slot, send_sem=s.at[d], recv_sem=r.at[d],
+            src_ref=slot, dst_ref=slot, send_sem=s, recv_sem=r,
             device_id={"pair": lax.rem(grp + d, npair)}, device_id_type=MESH,
         )
 
@@ -182,7 +187,7 @@
     k_in, k_out = iota((nb * wide_a, lanes), 0), iota((nb * wide_a, lanes), 1)
     k_at = lax.rem(k_out, group)
     source = (k_at // rows_a) * wide_a + start_a + lax.rem(k_at, rows_a)
-    pick = jnp.where((k_in == source) & (k_out < 2 * group), 1.0, 0.0).astype(BF16)
+    pick = jnp.where((k_in == source) & (k_out < group), 1.0, 0.0).astype(BF16)
 
     def overs(p):
         return cat([sa[p, k] for k in range(nb)], 1)
@@ -224,27 +229,24 @@
             copy.wait()
         base = dot(la[p], ra[p], 1, 1)
         tot[p] = base
-        bhl[p] = cat(halves(base), 0)
+        b16[p] = base.astype(BF16)
 
     pl.loop(0, count_a - DEPTH)(ladder)
     for p in range(count_a - DEPTH, count_a - 3):
         ladder(p)
 
-    lane_k = iota((wide_a, 2 * group), 1)
-    at_k = lax.rem(lane_k, group) // rows_a
+    at_k = iota((1, lanes), 1) // rows_a
     zero = jnp.zeros((rows_a, wide_a), F32)
+    rest = jnp.zeros((lanes - group, nb * wide_a), BF16)
 
     def couple(p):
-        rows, scale = [], jnp.zeros((wide_a, 2 * group), F32)
+        rows, scale = [], jnp.zeros((1, lanes), F32)
         for k in range(nb):
-            near = blk_a[nbr_a[k, p]].astype(F32)
-            rows.append(cat([near if i == k else zero for i in range(nb)], 1))
+            nbr = blk_a[nbr_a[k, p]].astype(F32)
+            rows.append(cat([nbr if i == k else zero for i in range(nb)], 1))
             scale = jnp.where(at_k == k, fock_a[k, p], scale)
-        rows = cat(rows, 0).astype(BF16)
-        right = dot(overs(p), cat([rows, rows], 0), 1, 1) * scale
-        high = right.astype(BF16).astype(F32)
-        right = jnp.where(lane_k < group, high, right - high).astype(BF16)
-        cpl[p] = dot(wsel[p][:, : 2 * group], right, 1, 1)
+        rows = cat([cat(rows, 0).astype(BF16), rest], 0)
+        near[p] = (dot(overs(p), rows, 1, 1) * scale).astype(BF16)
 
     fill = jnp.zeros((pad, wide_e), BF16)
     lane16, row16 = iota((16, lanes), 1), iota((16, lanes), 0)
@@ -264,56 +266,54 @@
         near = cat(halves(cat(parts, 0)), 0)
         return (base_h[h] + dot(wsel_e[h], near, 1, 0)).astype(BF16)
 
-    @pl.loop(1, npair)
-    def _(d):
-        to_pair(d, blk_a, count_a, blk_s, blk_r).wait()
-        to_pair(d, blk_e, count_e, ble_s, ble_r).wait()
-
-    for p in range(count_a // 2):
+    arrived(blk_a.at[pl.ds(0, (npair - 1) * count_a)], blk_s, blk_r)
+    arrived(blk_e.at[pl.ds(0, (npair - 1) * count_e)], ble_s, ble_r)
+
+    for p in range(count_a):
         couple(p)
-    ladder(7)
-    both_e = cat([couple_env(h) for h in range(count_e // 2)], 0)
-    srow, scol = iota((lanes, 2 * wide_e), 0), iota((lanes, 2 * wide_e), 1)
-    sj, sr = srow // 8, lax.rem(srow, 8)
-    si = lax.rem(sr, 4)
-    spread = jnp.where(
-        (scol == (sr // 4) * wide_e + rows_e * sj + si) & (si < rows_e), 1.0, 0.0
-    ).astype(BF16)
-    packed = dot(spread, both_e, 1, 0)
-    for j in range(naux):
-        send1[j, CHUNKS[1][1] - CHUNKS[1][0]] = packed[8 * j : 8 * j + 8].astype(BF16)
-    ladder(8)
-    for p in range(count_a // 2, count_a):
-        couple(p)
-    ladder(9)
-
     def sums_to(c, o):
         e = o[0] * nz + o[1]
         return pltpu.make_async_remote_copy(
             src_ref=sends[c].at[peer_of(o)], dst_ref=recvs[c].at[e],
-            send_sem=rs_s.at[c, e], recv_sem=rs_r.at[c, e],
+            send_sem=rs_s.at[c], recv_sem=rs_r.at[c],
             device_id={"aux": peer_of(o)}, device_id_type=MESH,
         )
 
     for c, (lo, hi) in enumerate(CHUNKS):
         if c == 0:
-            for o in far:
-                to_aux(o).wait()
+            arrived(gat.at[pl.ds(0, naux - 1)], gat_s, gat_r)
         for p in range(lo, hi):
             amp = gat[:, p].astype(F32).reshape(wide_a, wide_a).astype(BF16)
-            x = dot(cat([amp, amp], 0), bhl[p], 0, 0)
-            y = dot(cat(halves(x), 1), cat([amp, amp], 1), 1, 1)
-            total = (tot[p] + cpl[p] + x + y).reshape(naux, rows_a, wide_a)
+            x = dot(amp, b16[p], 0, 0)
+            y = dot(cat([x.astype(BF16), wsel[p]], 1), cat([amp, near[p]], 1), 1, 1)
+            total = (tot[p] + x + y).reshape(naux, rows_a, wide_a)
             sends[c][:, p - lo] = total.astype(BF16)
         for o in far:
             sums_to(c, o).start()
-
-    near_first = far[::-1]
+        if c == 0:
+            both_e = cat([couple_env(h) for h in range(count_e // 2)], 0)
+            srow, scol = iota((lanes, 2 * wide_e), 0), iota((lanes, 2 * wide_e), 1)
+            sj, sr = srow // 8, lax.rem(srow, 8)
+            si = lax.rem(sr, 4)
+            spread = jnp.where(
+                (scol == (sr // 4) * wide_e + rows_e * sj + si) & (si < rows_e), 1.0, 0.0
+            ).astype(BF16)
+            packed = dot(spread, both_e, 1, 0)
+            for j in range(naux):
+                send1[j, CHUNKS[1][1] - CHUNKS[1][0]] = packed[8 * j : 8 * j + 8].astype(BF16)
+            for p in range(count_a - 3, count_a):
+                for copy in load_pair(p):
+                    copy.wait()
+            for p in range(count_a - 3, count_a):
+                base = dot(la[p], ra[p], 1, 1)
+                tot[p] = base
+                b16[p] = base.astype(BF16)
+
     for c, (lo, hi) in enumerate(CHUNKS):
+        arrived(recvs[c].at[pl.ds(1, naux - 1)], rs_s.at[c], rs_r.at[c])
         acc = sends[c][me].astype(F32)
-        for o in near_first:
-            sums_to(c, o).wait()
-            acc = acc + recvs[c][o[0] * nz + o[1]].astype(F32)
+        for e in range(1, naux):
+            acc = acc + recvs[c][e].astype(F32)
         for p in range(lo, hi):
             out_a[p] = amp_a[p] - acc[p - lo] * rec_a[p]
         if c == 1:
@@ -369,8 +369,8 @@
             pltpu.VMEM((npair * count_a, rows_a, wide_a), BF16),
             pltpu.VMEM((npair * count_e, 8, 128), BF16),
             pltpu.VMEM((count_a, wide_a, wide_a), F32),
-            pltpu.VMEM((count_a, wide_a, wide_a), F32),
-            pltpu.VMEM((count_a, 2 * wide_a, wide_a), BF16),
+            pltpu.VMEM((count_a, wide_a, wide_a), BF16),
+            pltpu.VMEM((count_a, wide_a, wide_a), BF16),
             pltpu.VMEM((count_a, wide_a, 128), BF16),
             pltpu.VMEM((count_e // 2, wide_e, 128), BF16),
             pltpu.VMEM((count_a, rows_a, wide_a), F32),
@@ -382,9 +382,7 @@
             pltpu.VMEM((naux, n0, rows_a, wide_a), BF16),
             pltpu.VMEM((naux, n1 + 1, rows_a, wide_a), BF16),
             dma((12,)), dma((count_a,)), dma((count_a,)), dma, dma, dma, dma,
-            dma((naux,)), dma((naux,)),
-            dma((npair,)), dma((npair,)), dma((npair,)), dma((npair,)),
-            dma((2, naux)), dma((2, naux)),
+            dma, dma, dma, dma, dma, dma, dma((2,)), dma((2,)),
         ],
         compiler_params=pltpu.CompilerParams(
             collective_id=0, has_side_effects=True, vmem_limit_bytes=VMEM

time: 28.1 us -> 23.5 us (0.84)
  Pallas kernels: 26.1 us -> 21.5 us
    pallas_call x1, Pallas kernels: 26.1 us -> 21.5 us  [shards(): pl.pallas_call(functools.partial(kernel, npair, ny, nz), out_shape=(jax.S...]
where the time goes in v3:
time: 23.5 us; the launch traced here: 23.4 us
  Pallas kernels  21.5 us (91%)
  local copies, waits for them, and re-layouts  1.21 us (5%)
  between operations  0.65 us (3%)
    pallas_call x1, Pallas kernels, shards(): pl.pallas_call(functools.partial(kernel, npair, ny, nz), out_shape=(jax.S...  21.5 us
    unnamed x2, local copies, waits for them, and re-layouts  1.21 us

profile of v3, /device:TPU:0, one launch (start us, length us, event | category | flops | bytes accessed | tf_op | source)
XLA Modules:
  0.0 23.4 jit_solution(13151740529638843346)
XLA Ops:
  0.6 21.5 %shard_map.185 = (f32[10,8,128]{2,1,0:T(8,128)S(1)}, f32[3,4,48]{2,1,0:T(4,128)S(1)}) custom-call(s32[4,10]{1,0:T(4,128)} %bitcast.6, s32[10]{0:T(128)} %refs_1_.1, f32[4,10]{1,0:T(4,128)} %bitcast.7, f32[10]{0:T(128)} %refs_3_.1, s32[4,4]{1,0:T(4,128)} %refs_4_.1, s32[4]{0:T(128)} %refs_5_.1, f32[4,4]{1,0:T(4,128)} %refs_6_.1, f32[4]{0:T(128)} %refs_7_.1, ...), custom_call_target="tpu_custom_call" | custom-call | tf_op jit(solution)/shard_map/pallas_call | solution.py:351
  22.1 0.6 %copy.22 = f32[10,8,128]{2,1,0:T(8,128)} copy(f32[10,8,128]{2,1,0:T(8,128)S(1)} %get-tuple-element.8) | data formatting | bytes 81920
  22.8 0.6 %copy.23 = f32[4,3,48]{2,0,1:T(4,128)} copy(f32[4,3,48]{2,0,1:T(4,128)S(1)} %bitcast.4) | data formatting | bytes 4608

commit v4 on v3

--- a/solution.py
+++ b/solution.py
@@ -11,7 +11,7 @@
 F32, BF16, I32 = jnp.float32, jnp.bfloat16, jnp.int32
 FIRST, DEPTH = 2, 5
 VMEM = 36 * 1024 * 1024
-CHUNKS = ((0, 5), (5, 10))
+CHUNKS = ((0, 6), (6, 10))
 
 
 def halves(x):
@@ -49,7 +49,7 @@
     la_hbm, ra_hbm, sa_hbm, le_hbm, re_hbm, se_hbm,
     out_a, out_e,
     la, ra, sa, le, re, se,
-    gat, blk_a, blk_e, tot, b16, near, wsel, wsel_e, amp_a, rec_a, amp_e, rec_e,
+    gat0, gat1, blk_a, blk_e, tot, b16, near, ampb, turn, wsel, wsel_e, amp_a, rec_a, amp_e, rec_e,
     send0, send1, recv0, recv1,
     small_sem, la_sem, ra_sem, le_sem, re_sem, sa_sem, se_sem,
     gat_s, gat_r, blk_s, blk_r, ble_s, ble_r, rs_s, rs_r,
@@ -64,6 +64,7 @@
     nb = nbr_a.shape[0]
     lanes = wide_a
     start_a, start_e = me * rows_a, me * rows_e
+    gats = (gat0, gat1)
     sends, recvs = (send0, send1), (recv0, recv1)
 
     far = sorted(
@@ -120,7 +121,8 @@
         own = jnp.where(inside, amps_a[p].astype(F32), 0.0)
         amp_a[p] = own
         own = own.astype(BF16)
-        gat[me, p] = own
+        c = 0 if p < CHUNKS[0][1] else 1
+        gats[c][me, p - CHUNKS[c][0]] = own
         blk_a[grp * count_a + p] = own
 
     def own_env(q):
@@ -139,10 +141,10 @@
 
     pl.semaphore_wait(barrier, naux + npair - 2)
 
-    def to_aux(o):
-        slot = gat.at[me]
+    def to_aux(c, o):
+        slot = gats[c].at[me]
         return pltpu.make_async_remote_copy(
-            src_ref=slot, dst_ref=slot, send_sem=gat_s, recv_sem=gat_r,
+            src_ref=slot, dst_ref=slot, send_sem=gat_s.at[c], recv_sem=gat_r.at[c],
             device_id={"aux": peer_of(o)}, device_id_type=MESH,
         )
 
@@ -162,8 +164,9 @@
     for d in range(1, npair):
         to_pair(d, blk_a, count_a, blk_s, blk_r).start()
         to_pair(d, blk_e, count_e, ble_s, ble_r).start()
-    for o in far:
-        to_aux(o).start()
+    for c in range(2):
+        for o in far:
+            to_aux(c, o).start()
 
     for p in range(FIRST, DEPTH):
         start_pair(p)
@@ -232,7 +235,7 @@
         b16[p] = base.astype(BF16)
 
     pl.loop(0, count_a - DEPTH)(ladder)
-    for p in range(count_a - DEPTH, count_a - 3):
+    for p in range(count_a - DEPTH, 7):
         ladder(p)
 
     at_k = iota((1, lanes), 1) // rows_a
@@ -281,16 +284,26 @@
 
     for c, (lo, hi) in enumerate(CHUNKS):
         if c == 0:
-            arrived(gat.at[pl.ds(0, naux - 1)], gat_s, gat_r)
+            arrived(gat0.at[pl.ds(0, naux - 1)], gat_s.at[0], gat_r.at[0])
+        if c == 0:
+            pass
         for p in range(lo, hi):
-            amp = gat[:, p].astype(F32).reshape(wide_a, wide_a).astype(BF16)
-            x = dot(amp, b16[p], 0, 0)
+            if c == 0:
+                amp = gat0[:, p].astype(F32).reshape(wide_a, wide_a).astype(BF16)
+                x = dot(amp, b16[p], 0, 0)
+            else:
+                amp = gat1[:, p - lo].astype(F32).reshape(wide_a, wide_a).astype(BF16)
+                x = dot(amp, b16[p], 0, 0)
             y = dot(cat([x.astype(BF16), wsel[p]], 1), cat([amp, near[p]], 1), 1, 1)
             total = (tot[p] + x + y).reshape(naux, rows_a, wide_a)
             sends[c][:, p - lo] = total.astype(BF16)
         for o in far:
             sums_to(c, o).start()
         if c == 0:
+            arrived(gat1.at[pl.ds(0, naux - 1)], gat_s.at[1], gat_r.at[1])
+            for p in (7, 8):
+                for copy in load_pair(p):
+                    copy.wait()
             both_e = cat([couple_env(h) for h in range(count_e // 2)], 0)
             srow, scol = iota((lanes, 2 * wide_e), 0), iota((lanes, 2 * wide_e), 1)
             sj, sr = srow // 8, lax.rem(srow, 8)
@@ -301,10 +314,14 @@
             packed = dot(spread, both_e, 1, 0)
             for j in range(naux):
                 send1[j, CHUNKS[1][1] - CHUNKS[1][0]] = packed[8 * j : 8 * j + 8].astype(BF16)
-            for p in range(count_a - 3, count_a):
+            for p in (7, 8):
+                base = dot(la[p], ra[p], 1, 1)
+                tot[p] = base
+                b16[p] = base.astype(BF16)
+            for p in (9,):
                 for copy in load_pair(p):
                     copy.wait()
-            for p in range(count_a - 3, count_a):
+            for p in (9,):
                 base = dot(la[p], ra[p], 1, 1)
                 tot[p] = base
                 b16[p] = base.astype(BF16)
@@ -325,6 +342,17 @@
                 new = amp_e[q][:4] - block * rec_e[q][:4]
                 for i in range(rows_e):
                     out_e[i, q : q + 1, :] = new[i : i + 1]
+
+
+def hand_over(from_a, from_e, out_a, out_e, sem):
+    copies = (
+        pltpu.make_async_copy(from_a, out_a, sem.at[0]),
+        pltpu.make_async_copy(from_e, out_e, sem.at[1]),
+    )
+    for copy in copies:
+        copy.start()
+    for copy in copies:
+        copy.wait()
 
 
 def shards(
@@ -348,7 +376,7 @@
         neighbor_env, rank_env, fock_env, gap_env,
         amps_active, energy_active, amps_env.transpose(1, 0, 2), energy_env,
     )
-    new_active, new_env = pl.pallas_call(
+    sums = pl.pallas_call(
         functools.partial(kernel, npair, ny, nz),
         out_shape=(
             jax.ShapeDtypeStruct((count_a, rows_a, wide_a), F32),
@@ -365,12 +393,15 @@
             pltpu.VMEM(left_env.shape, BF16),
             pltpu.VMEM(right_env.shape, BF16),
             pltpu.VMEM(intersect_env.shape, BF16),
-            pltpu.VMEM((naux, count_a, rows_a, wide_a), BF16),
+            pltpu.VMEM((naux, n0, rows_a, wide_a), BF16),
+            pltpu.VMEM((naux, n1, rows_a, wide_a), BF16),
             pltpu.VMEM((npair * count_a, rows_a, wide_a), BF16),
             pltpu.VMEM((npair * count_e, 8, 128), BF16),
             pltpu.VMEM((count_a, wide_a, wide_a), F32),
             pltpu.VMEM((count_a, wide_a, wide_a), BF16),
             pltpu.VMEM((count_a, wide_a, wide_a), BF16),
+            pltpu.VMEM((n1, wide_a, wide_a), BF16),
+            pltpu.VMEM((n1, wide_a, wide_a), BF16),
             pltpu.VMEM((count_a, wide_a, 128), BF16),
             pltpu.VMEM((count_e // 2, wide_e, 128), BF16),
             pltpu.VMEM((count_a, rows_a, wide_a), F32),
@@ -382,7 +413,7 @@
             pltpu.VMEM((naux, n0, rows_a, wide_a), BF16),
             pltpu.VMEM((naux, n1 + 1, rows_a, wide_a), BF16),
             dma((12,)), dma((count_a,)), dma((count_a,)), dma, dma, dma, dma,
-            dma, dma, dma, dma, dma, dma, dma((2,)), dma((2,)),
+            dma((2,)), dma((2,)), dma, dma, dma, dma, dma((2,)), dma((2,)),
         ],
         compiler_params=pltpu.CompilerParams(
             collective_id=0, has_side_effects=True, vmem_limit_bytes=VMEM
@@ -394,6 +425,17 @@
             + (left_active, right_active, intersect_active, left_env, right_env, intersect_env)
         )
     )
+    new_active, new_env = pl.pallas_call(
+        hand_over,
+        out_shape=(
+            jax.ShapeDtypeStruct((count_a, rows_a, wide_a), F32),
+            jax.ShapeDtypeStruct((rows_e, count_e, wide_e), F32),
+        ),
+        in_specs=[vmem, vmem],
+        out_specs=(hbm, hbm),
+        scratch_shapes=[dma((2,))],
+        compiler_params=pltpu.CompilerParams(vmem_limit_bytes=8 * 1024 * 1024),
+    )(*sums)
     return new_active, new_env.transpose(1, 0, 2)
 
 

time: 23.5 us -> 22.5 us (0.957)
  local copies, waits for them, and re-layouts: 1.21 us -> 0 us
  Pallas kernels: 21.5 us -> 21.8 us
    unnamed x2 -> x0, local copies, waits for them, and re-layouts: 1.21 us -> none
    pallas_call x0 -> x1, Pallas kernels: none -> 0.64 us  [shards(): pl.pallas_call(hand_over, out_shape=(jax.ShapeDtypeStruct((count_a, rows_...]
    pallas_call x1, Pallas kernels: 21.5 us -> 21.1 us  [shards(): pl.pallas_call(functools.partial(kernel, npair, ny, nz), out_shape=(jax.S...]
where the time goes in v4:
time: 22.5 us; the launch traced here: 22.4 us
  Pallas kernels  21.8 us (97%)
  between operations  0.65 us (3%)
    pallas_call x1, Pallas kernels, shards(): pl.pallas_call(functools.partial(kernel, npair, ny, nz), out_shape=(jax.S...  21.1 us
    pallas_call x1, Pallas kernels, shards(): pl.pallas_call(hand_over, out_shape=(jax.ShapeDtypeStruct((count_a, rows_...  0.64 us

profile of v4, /device:TPU:0, one launch (start us, length us, event | category | flops | bytes accessed | tf_op | source)
XLA Modules:
  0.0 22.4 jit_solution(13697428699191435827)
XLA Ops:
  0.6 21.1 %shard_map.185 = (f32[10,8,128]{2,1,0:T(8,128)S(1)}, f32[3,4,48]{2,1,0:T(4,128)S(1)}) custom-call(s32[4,10]{1,0:T(4,128)} %bitcast.5, s32[10]{0:T(128)} %refs_1_.1, f32[4,10]{1,0:T(4,128)} %bitcast.6, f32[10]{0:T(128)} %refs_3_.1, s32[4,4]{1,0:T(4,128)} %refs_4_.1, s32[4]{0:T(128)} %refs_5_.1, f32[4,4]{1,0:T(4,128)} %refs_6_.1, f32[4]{0:T(128)} %refs_7_.1, ...), custom_call_target="tpu_custom_call" | custom-call | tf_op jit(solution)/shard_map/pallas_call | solution.py:379
  21.8 0.6 %shard_map.186 = (f32[10,8,128]{2,1,0:T(8,128)}, f32[3,4,48]{2,1,0:T(4,128)}) custom-call(f32[10,8,128]{2,1,0:T(8,128)S(1)} %get-tuple-element.6.from_a, f32[3,4,48]{2,1,0:T(4,128)S(1)} %get-tuple-element.7.from_e), custom_call_target="tpu_custom_call" | custom-call | tf_op jit(solution)/shard_map/pallas_call | solution.py:428

commit v5 on v4

--- a/solution.py
+++ b/solution.py
@@ -161,12 +161,13 @@
             device_id={"pair": lax.rem(grp + d, npair)}, device_id_type=MESH,
         )
 
-    for d in range(1, npair):
-        to_pair(d, blk_a, count_a, blk_s, blk_r).start()
-        to_pair(d, blk_e, count_e, ble_s, ble_r).start()
     for c in range(2):
         for o in far:
             to_aux(c, o).start()
+        if c == 0:
+            for d in range(1, npair):
+                to_pair(d, blk_a, count_a, blk_s, blk_r).start()
+                to_pair(d, blk_e, count_e, ble_s, ble_r).start()
 
     for p in range(FIRST, DEPTH):
         start_pair(p)
@@ -211,6 +212,16 @@
                 chosen = chosen + dot(se[2 * h + b, k], sel, 1, 0)
         wsel_e[h] = chosen.astype(BF16)
 
+    def ladder(p):
+        if not isinstance(p, int):
+            start_pair(p + DEPTH)
+        for copy in load_pair(p):
+            copy.wait()
+        base = dot(la[p], ra[p], 1, 1)
+        tot[p] = base
+        b16[p] = base.astype(BF16)
+
+    pl.loop(0, 2)(ladder)
     for copy in load_env:
         copy.wait()
     le_all = le[...].reshape(count_e * wide_e, le.shape[2])
@@ -225,16 +236,7 @@
         a, b = 2 * h * wide_e, (2 * h + 1) * wide_e
         base_h.append(jnp.where(low_lanes, block[a : a + wide_e], block[b : b + wide_e]))
 
-    def ladder(p):
-        if not isinstance(p, int):
-            start_pair(p + DEPTH)
-        for copy in load_pair(p):
-            copy.wait()
-        base = dot(la[p], ra[p], 1, 1)
-        tot[p] = base
-        b16[p] = base.astype(BF16)
-
-    pl.loop(0, count_a - DEPTH)(ladder)
+    pl.loop(2, count_a - DEPTH)(ladder)
     for p in range(count_a - DEPTH, 7):
         ladder(p)
 

time: 22.5 us -> 22.5 us (level)
  no operation moved by 1% of the time
where the time goes in v5:
time: 22.5 us; the launch traced here: 22.4 us
  Pallas kernels  21.8 us (97%)
  between operations  0.65 us (3%)
    pallas_call x1, Pallas kernels, shards(): pl.pallas_call(functools.partial(kernel, npair, ny, nz), out_shape=(jax.S...  21.1 us
    pallas_call x1, Pallas kernels, shards(): pl.pallas_call(hand_over, out_shape=(jax.ShapeDtypeStruct((count_a, rows_...  0.64 us

profile of v5, /device:TPU:0, one launch (start us, length us, event | category | flops | bytes accessed | tf_op | source)
XLA Modules:
  0.0 22.4 jit_solution(12849122056581555574)
XLA Ops:
  0.6 21.1 %shard_map.185 = (f32[10,8,128]{2,1,0:T(8,128)S(1)}, f32[3,4,48]{2,1,0:T(4,128)S(1)}) custom-call(s32[4,10]{1,0:T(4,128)} %bitcast.5, s32[10]{0:T(128)} %refs_1_.1, f32[4,10]{1,0:T(4,128)} %bitcast.6, f32[10]{0:T(128)} %refs_3_.1, s32[4,4]{1,0:T(4,128)} %refs_4_.1, s32[4]{0:T(128)} %refs_5_.1, f32[4,4]{1,0:T(4,128)} %refs_6_.1, f32[4]{0:T(128)} %refs_7_.1, ...), custom_call_target="tpu_custom_call" | custom-call | tf_op jit(solution)/shard_map/pallas_call | solution.py:381
  21.8 0.6 %shard_map.186 = (f32[10,8,128]{2,1,0:T(8,128)}, f32[3,4,48]{2,1,0:T(4,128)}) custom-call(f32[10,8,128]{2,1,0:T(8,128)S(1)} %get-tuple-element.6.from_a, f32[3,4,48]{2,1,0:T(4,128)S(1)} %get-tuple-element.7.from_e), custom_call_target="tpu_custom_call" | custom-call | tf_op jit(solution)/shard_map/pallas_call | solution.py:430
